TPU v7x, 32 devices: a whole 2x2x4 slice. The times are simulated.
32 devices in a mesh: fsdp: 2 (over y), ctx: 4 (over x, core), tp: 4 (over z).
Axes of the slice: x: 2, y: 2, z: 4, core: 2. Of those that a mesh axis runs over, the one named last changes fastest.
Arguments:
- block_input: bfloat16 [4, 2048, 1024], P('fsdp', 'ctx'), may hold values from -6 to 6
- positions: int32 [3, 4, 2048], P(None, 'fsdp', 'ctx'), may hold values from 0 to 15
- w_qkv: bfloat16 [3, 1024, 1024], P(None, 'fsdp', 'tp'), may hold values from -0.1875 to 0.1875
- b_qkv: float32 [3, 1024], P(None, 'tp'), may hold values from -3 to 3
- w_proj: bfloat16 [1024, 1024], P('tp', 'fsdp'), may hold values from -1 to 1
- w_up: bfloat16 [1024, 4096], P('fsdp', 'tp'), may hold values from -0.1875 to 0.1875
- b_up: float32 [4096], P('tp'), may hold values from -3 to 3
- w_down: bfloat16 [4096, 1024], P('tp', 'fsdp'), may hold values from -0.09375 to 0.09375
- norm_gains: float32 [2, 1024], replicated, may hold values from 0.5 to 1.5
- norm_shifts: float32 [2, 1024], replicated, may hold values from -2 to 2
- out_shifts: float32 [2, 1024], replicated, may hold values from -2 to 2
- grad_out: bfloat16 [4, 2048, 1024], P('fsdp', 'ctx'), may hold values from -6 to 6
Outputs:
- block_output: bfloat16 [4, 2048, 1024], P('fsdp', 'ctx')
- grad_input: float32 [4, 2048, 1024], P('fsdp', 'ctx')
- grad_w_qkv: float32 [3, 1024, 1024], P(None, 'fsdp', 'tp')
- grad_b_qkv: float32 [3, 1024], P(None, 'tp')
- grad_w_proj: float32 [1024, 1024], P('tp', 'fsdp')
- grad_w_up: float32 [1024, 4096], P('fsdp', 'tp')
- grad_b_up: float32 [4096], P('tp')
- grad_w_down: float32 [4096, 1024], P('tp', 'fsdp')
- grad_gains: float32 [2, 1024], replicated
- grad_shifts: float32 [2, 1024], replicated
- grad_out_shifts: float32 [2, 1024], replicated
Inputs may be any that keep to these rules, and one draw needn't show every extreme that they name: `positions`: each token's time, height and width index in its clip.
All inputs are finite; a program needn't handle non-finite values.
Results may differ from a plain program's by a relative error of at most 0.02.
Values may be sent and summed in bfloat16 or wider, within the bound.
A program may use at most 128 MiB of HBM per device.

v0:
```python
from functools import partial
import jax
import jax.numpy as jnp
from jax import lax
from jax.sharding import PartitionSpec as P

HD = 64
LEN = 2048
ROT = 20
QBLK = 512
EPSILON = 1e-06


def layer_norm(values, gain_vec, shift_vec):
    center = values - jnp.mean(values, axis=-1, keepdims=True)
    spread = jnp.mean(center * center, axis=-1, keepdims=True)
    return center * lax.rsqrt(spread + EPSILON) * gain_vec + shift_vec


def rotary_tables(position_rows):
    half_rot = ROT // 2
    freqs = 10000.0 ** (-2.0 * jnp.arange(half_rot, dtype=jnp.float32) / ROT)
    angles = position_rows.astype(jnp.float32)[:, :, None] * freqs[None, None, :]
    return (jnp.cos(angles), jnp.sin(angles))


def rotary(values, cos_table, sin_table):
    half_rot = ROT // 2
    pieces = []
    for dim_index in range(3):
        offset_at = dim_index * ROT
        first_half = values[..., offset_at : offset_at + half_rot]
        second_half = values[..., offset_at + half_rot : offset_at + ROT]
        cos_part = cos_table[dim_index][:, None, :]
        sin_part = sin_table[dim_index][:, None, :]
        pieces.append(first_half * cos_part - second_half * sin_part)
        pieces.append(second_half * cos_part + first_half * sin_part)
    pieces.append(values[..., 3 * ROT :])
    return jnp.concatenate(pieces, axis=-1)


def contract_rows(left_mat, right_mat):
    return lax.dot_general(
        left_mat, right_mat, (((0,), (0,)), ((), ())), preferred_element_type=jnp.float32
    )


def contract_cols(left_mat, right_mat):
    return lax.dot_general(
        left_mat, right_mat, (((1,), (1,)), ((), ())), preferred_element_type=jnp.float32
    )


def tp_whole(partial_sum):
    return lax.psum(partial_sum.astype(jnp.bfloat16), "tp").astype(jnp.float32)


def attend_group(operands):
    queries, keys_all, values_all = operands
    score_factor = HD ** (-0.5)

    def attend_block(query_block):
        scores = (
            jnp.einsum("qe,ke->qk", query_block, keys_all, preferred_element_type=jnp.float32)
            * score_factor
        )
        largest = jnp.max(scores, axis=-1, keepdims=True)
        expon = jnp.exp(scores - largest)
        totals = jnp.sum(expon, axis=-1, keepdims=True)
        probs = expon / totals
        block_out = jnp.dot(
            probs.astype(jnp.bfloat16), values_all, preferred_element_type=jnp.float32
        )
        return (block_out.astype(jnp.bfloat16), (largest + jnp.log(totals))[:, 0])

    return lax.map(attend_block, queries.reshape(LEN // QBLK, QBLK, HD))


def backward_group(operands):
    queries, keys_all, values_all, grad_attended, log_totals = operands
    score_factor = HD ** (-0.5)

    def back_block(carry, block_items):
        grad_keys, grad_values = carry
        query_block, grad_block, log_block = block_items
        scores = (
            jnp.einsum("qe,ke->qk", query_block, keys_all, preferred_element_type=jnp.float32)
            * score_factor
        )
        probs = jnp.exp(scores - log_block[:, None])
        probs_low = probs.astype(jnp.bfloat16)
        grad_probs = jnp.einsum(
            "qe,ke->qk", grad_block, values_all, preferred_element_type=jnp.float32
        )
        inner = jnp.sum(probs * grad_probs, axis=-1, keepdims=True)
        grad_scores = (probs * (grad_probs - inner)).astype(jnp.bfloat16)
        grad_query = (
            jnp.dot(grad_scores, keys_all, preferred_element_type=jnp.float32) * score_factor
        )
        grad_keys = grad_keys + contract_rows(grad_scores, query_block) * score_factor
        grad_values = grad_values + contract_rows(probs_low, grad_block)
        return ((grad_keys, grad_values), grad_query)

    zeros_kv = jnp.zeros((LEN, HD), jnp.float32)
    block_count = LEN // QBLK
    items = (
        queries.reshape(block_count, QBLK, HD),
        grad_attended.reshape(block_count, QBLK, HD),
        log_totals,
    )
    (grad_keys, grad_values), grad_queries = lax.scan(back_block, (zeros_kv, zeros_kv), items)
    return (grad_queries.reshape(LEN, HD), grad_keys, grad_values)


def shards(
    block_input,
    positions,
    w_qkv,
    b_qkv,
    w_proj,
    w_up,
    b_up,
    w_down,
    norm_gains,
    norm_shifts,
    out_shifts,
    grad_out,
):
    clip_count, local_len, width = block_input.shape
    row_count = clip_count * local_len
    ctx_count = lax.axis_size("ctx")
    local_width = w_qkv.shape[2]
    group_heads = local_width // ctx_count // HD
    group_count = clip_count * group_heads
    inputs = block_input.reshape(row_count, width).astype(jnp.float32)
    full_qkv, full_proj, full_up, full_down = (
        lax.all_gather(w_qkv, "fsdp", axis=1, tiled=True),
        lax.all_gather(w_proj, "fsdp", axis=1, tiled=True),
        lax.all_gather(w_up, "fsdp", axis=0, tiled=True),
        lax.all_gather(w_down, "fsdp", axis=1, tiled=True),
    )
    cos_table, sin_table = rotary_tables(positions.reshape(3, row_count))
    normed_one = layer_norm(inputs, norm_gains[0], norm_shifts[0])
    normed_one_low = normed_one.astype(jnp.bfloat16)
    projected = (
        jnp.einsum("rd,cde->cre", normed_one_low, full_qkv, preferred_element_type=jnp.float32)
        + b_qkv[:, None, :]
    )
    head_shape = (row_count, local_width // HD, HD)
    queries_rot = rotary(projected[0].reshape(head_shape), cos_table, sin_table).reshape(
        row_count, local_width
    )
    keys_rot = rotary(projected[1].reshape(head_shape), cos_table, sin_table).reshape(
        row_count, local_width
    )
    token_qkv = (
        jnp.stack([queries_rot, keys_rot, projected[2]])
        .astype(jnp.bfloat16)
        .reshape(3, clip_count, local_len, local_width)
    )
    head_qkv = lax.all_to_all(token_qkv, "ctx", split_axis=3, concat_axis=2, tiled=True)
    full_len = head_qkv.shape[2]
    grouped = (
        head_qkv.reshape(3, clip_count, full_len, group_heads, HD)
        .transpose(0, 1, 3, 2, 4)
        .reshape(3, group_count, full_len, HD)
    )
    attended, log_totals = lax.map(attend_group, (grouped[0], grouped[1], grouped[2]))
    attended = (
        attended.reshape(clip_count, group_heads, full_len, HD)
        .transpose(0, 2, 1, 3)
        .reshape(clip_count, full_len, group_heads * HD)
    )
    token_attended = lax.all_to_all(
        attended, "ctx", split_axis=1, concat_axis=2, tiled=True
    ).reshape(row_count, local_width)
    attn_part = jnp.dot(token_attended, full_proj, preferred_element_type=jnp.float32)
    residual = inputs + tp_whole(attn_part) + out_shifts[0]
    normed_two_low = layer_norm(residual, norm_gains[1], norm_shifts[1]).astype(jnp.bfloat16)
    pre_act = jnp.dot(normed_two_low, full_up, preferred_element_type=jnp.float32) + b_up
    act_low = jax.nn.gelu(pre_act, approximate=False).astype(jnp.bfloat16)
    mlp_part = jnp.dot(act_low, full_down, preferred_element_type=jnp.float32)
    result = residual + tp_whole(mlp_part) + out_shifts[1]
    block_rows = result.astype(jnp.bfloat16)
    full_qkv, full_proj, full_up, full_down = (
        lax.all_gather(w_qkv, "fsdp", axis=1, tiled=True),
        lax.all_gather(w_proj, "fsdp", axis=1, tiled=True),
        lax.all_gather(w_up, "fsdp", axis=0, tiled=True),
        lax.all_gather(w_down, "fsdp", axis=1, tiled=True),
    )
    upstream = grad_out.reshape(row_count, width).astype(jnp.float32)
    upstream_low = upstream.astype(jnp.bfloat16)
    grad_down = contract_rows(act_low, upstream_low)
    grad_act = contract_cols(upstream_low, full_down)
    _, gelu_pull = jax.vjp(partial(jax.nn.gelu, approximate=False), pre_act)
    grad_pre = gelu_pull(grad_act)[0].astype(jnp.bfloat16)
    grad_b_up = jnp.sum(grad_pre.astype(jnp.float32), axis=0)
    grad_up = contract_rows(normed_two_low, grad_pre)
    back_part_two = contract_cols(grad_pre, full_up)
    grad_normed_two = tp_whole(back_part_two)
    _, norm_pull_two = jax.vjp(layer_norm, residual, norm_gains[1], norm_shifts[1])
    grad_res_norm, grad_gain_two, grad_shift_two = norm_pull_two(grad_normed_two)
    grad_residual = upstream + grad_res_norm
    grad_residual_low = grad_residual.astype(jnp.bfloat16)
    grad_proj = contract_rows(token_attended, grad_residual_low)
    grad_token_att = (
        contract_cols(grad_residual_low, full_proj)
        .astype(jnp.bfloat16)
        .reshape(clip_count, local_len, local_width)
    )
    grad_head_att = lax.all_to_all(grad_token_att, "ctx", split_axis=2, concat_axis=1, tiled=True)
    grad_grouped = (
        grad_head_att.reshape(clip_count, full_len, group_heads, HD)
        .transpose(0, 2, 1, 3)
        .reshape(group_count, full_len, HD)
    )
    grad_q, grad_k, grad_v = lax.map(
        backward_group, (grouped[0], grouped[1], grouped[2], grad_grouped, log_totals)
    )
    grad_heads = jnp.stack([grad_q, grad_k, grad_v]).astype(jnp.bfloat16)
    grad_heads = (
        grad_heads.reshape(3, clip_count, group_heads, full_len, HD)
        .transpose(0, 1, 3, 2, 4)
        .reshape(3, clip_count, full_len, group_heads * HD)
    )
    grad_tokens = (
        lax.all_to_all(grad_heads, "ctx", split_axis=2, concat_axis=3, tiled=True)
        .reshape(3, row_count, local_width)
        .astype(jnp.float32)
    )

    def rotate_rows(moved):
        return rotary(moved, cos_table, sin_table)

    _, rotary_pull = jax.vjp(rotate_rows, jnp.zeros(head_shape, jnp.float32))
    grad_q_pre = rotary_pull(grad_tokens[0].reshape(head_shape))[0].reshape(row_count, local_width)
    grad_k_pre = rotary_pull(grad_tokens[1].reshape(head_shape))[0].reshape(row_count, local_width)
    grad_qkv_low = jnp.stack([grad_q_pre, grad_k_pre, grad_tokens[2]]).astype(jnp.bfloat16)
    grad_b_qkv = jnp.sum(grad_qkv_low.astype(jnp.float32), axis=1)
    grad_qkv = jnp.einsum(
        "rd,cre->cde", normed_one_low, grad_qkv_low, preferred_element_type=jnp.float32
    )
    back_part_one = jnp.einsum(
        "cre,cde->rd", grad_qkv_low, full_qkv, preferred_element_type=jnp.float32
    )
    grad_normed_one = tp_whole(back_part_one)
    _, norm_pull_one = jax.vjp(layer_norm, inputs, norm_gains[0], norm_shifts[0])
    grad_in_norm, grad_gain_one, grad_shift_one = norm_pull_one(grad_normed_one)
    grad_input_rows = grad_residual + grad_in_norm
    norm_vectors = jnp.stack(
        [
            grad_gain_one,
            grad_gain_two,
            grad_shift_one,
            grad_shift_two,
            jnp.sum(grad_residual, axis=0),
            jnp.sum(upstream, axis=0),
        ]
    )
    block_output = block_rows.reshape(clip_count, local_len, width)
    grad_input = grad_input_rows.reshape(clip_count, local_len, width)
    shard_qkv, shard_proj, shard_up, shard_down = (
        lax.psum_scatter(
            grad_qkv.astype(jnp.bfloat16), "fsdp", scatter_dimension=1, tiled=True
        ).astype(jnp.float32),
        lax.psum_scatter(
            grad_proj.astype(jnp.bfloat16), "fsdp", scatter_dimension=1, tiled=True
        ).astype(jnp.float32),
        lax.psum_scatter(
            grad_up.astype(jnp.bfloat16), "fsdp", scatter_dimension=0, tiled=True
        ).astype(jnp.float32),
        lax.psum_scatter(
            grad_down.astype(jnp.bfloat16), "fsdp", scatter_dimension=1, tiled=True
        ).astype(jnp.float32),
    )
    shard_qkv, shard_proj, shard_up, shard_down = (
        lax.psum(shard_qkv.astype(jnp.bfloat16), "ctx").astype(jnp.float32),
        lax.psum(shard_proj.astype(jnp.bfloat16), "ctx").astype(jnp.float32),
        lax.psum(shard_up.astype(jnp.bfloat16), "ctx").astype(jnp.float32),
        lax.psum(shard_down.astype(jnp.bfloat16), "ctx").astype(jnp.float32),
    )
    gains_sum, shifts_sum, outs_sum, bqkv_sum, bup_sum = lax.psum(
        (norm_vectors[0:2], norm_vectors[2:4], norm_vectors[4:6], grad_b_qkv, grad_b_up),
        ("fsdp", "ctx"),
    )
    return (
        block_output,
        grad_input,
        shard_qkv,
        bqkv_sum,
        shard_proj,
        shard_up,
        bup_sum,
        shard_down,
        gains_sum,
        shifts_sum,
        outs_sum,
    )


def solution(mesh):
    in_specs = (
        P("fsdp", "ctx", None),
        P(None, "fsdp", "ctx"),
        P(None, "fsdp", "tp"),
        P(None, "tp"),
        P("tp", "fsdp"),
        P("fsdp", "tp"),
        P("tp"),
        P("tp", "fsdp"),
        P(),
        P(),
        P(),
        P("fsdp", "ctx", None),
    )
    out_specs = (
        P("fsdp", "ctx", None),
        P("fsdp", "ctx", None),
        P(None, "fsdp", "tp"),
        P(None, "tp"),
        P("tp", "fsdp"),
        P("fsdp", "tp"),
        P("tp"),
        P("tp", "fsdp"),
        P(),
        P(),
        P(),
    )
    return jax.shard_map(shards, mesh=mesh, in_specs=in_specs, out_specs=out_specs, check_vma=False)
```

profile of v0, /device:TPU:0, one launch (start us, length us, event | category | flops | bytes accessed | tf_op | source)
XLA Modules:
  0.0 875.1 jit_solution(13437522062420596701)
XLA Ops:
  7.3 2.4 copy.73
  9.7 1.9 convert_reduce_fusion.2
  15.1 2.1 fusion.40
  17.3 22.8 %all-gather.4.cloned.1.call-done = bf16[3,1024,256]{1,2,0:T(8,128)(2,1)} async-done(((bf16[3,512,256]{1,2,0:T(8,128)(2,1)}), bf16[3,1024,256]{1,2,0:T(8,128)(2,1)}) %all-gather.4.cloned.1.call-update) | async-done | bytes 1572880 | tf_op jit(solution)/shard_map/all_gather | solution.py:137
  40.1 3.9 add_bitcast_fusion
  46.6 2.1 concatenate.14
  49.0 2.1 concatenate.13
  51.5 3.1 pad_maximum_fusion.1
  54.5 3.8 all-to-all-start
  58.3 20.0 %all-to-all-done = bf16[3,2,512,256]{2,1,0,3:T(2,128)(2,1)S(1)} async-done(((bf16[3,2,512,256]{2,1,0,3:T(2,128)(2,1)}), bf16[3,2,512,256]{2,1,0,3:T(2,128)(2,1)S(1)}, u32[]{:S(2)}, u32[]{:S(2)}) %all-to-all-start) | async-done | bytes 1572896 | tf_op jit(solution)/shard_map/all_to_all | solution.py:161
  83.0 27.2 %while.54 = (s32[]{:T(128)}, bf16[2,4,512,64]{2,3,1,0:T(8,128)(2,1)}, f32[2,4,512]{2,1,0:T(4,128)S(1)}, bf16[2,2048,64]{2,1,0:T(8,128)(2,1)S(1)}, bf16[2,2048,64...) while((s32[]{:T(128)}, ...), condition=%wide.region_7.8_spmd, body=%wide.region_2.7_spmd.sunk | while | flops 277904896 | bytes 20156772 | solution.py:168
  84.4 11.4 %while.57 = (s32[]{:T(128)}, bf16[4,512,64]{1,2,0:T(8,128)(2,1)S(1)}, f32[4,512]{1,0:T(4,128)S(1)}, bf16[4,512,64]{2,1,0:T(8,128)(2,1)S(1)}, bf16[2048,64]{1,0:T...) while((s32[]{:T(128)}, bf16[4,512,64]{1,2,0:T(8,128)(2,1)S(1)}, ...), condition=%wide.region_6.6_spmd, body=%wide.region_3.5_spmd.sunk | while | flops 277904896 | bytes 13848681 | solution.py:76
  98.0 11.4 %while.57 = (s32[]{:T(128)}, bf16[4,512,64]{1,2,0:T(8,128)(2,1)S(1)}, f32[4,512]{1,0:T(4,128)S(1)}, bf16[4,512,64]{2,1,0:T(8,128)(2,1)S(1)}, bf16[2048,64]{1,0:T...) while((s32[]{:T(128)}, bf16[4,512,64]{1,2,0:T(8,128)(2,1)S(1)}, ...), condition=%wide.region_6.6_spmd, body=%wide.region_3.5_spmd.sunk | while | flops 277904896 | bytes 13848681 | solution.py:76
  110.3 2.6 copy.101
  114.4 3.5 all-to-all-start.1
  117.9 9.3 %all_gather.17 = bf16[256,1024]{1,0:T(8,128)(2,1)S(1)} all-gather(bf16[256,512]{1,0:T(8,128)(2,1)S(1)} %copy-done.30), channel_id=1, replica_groups=mesh['fsdp'=2,'ctx'=4,'tp'=4] {'fsdp'}, dimensions={1}, use_global_device_ids=true | all-gather | bytes 786432 | tf_op jit(solution)/shard_map/all_gather | solution.py:138
  128.0 1.9 copy.82
  131.1 2.1 convolution_convert_fusion.4
  135.5 84.2 %all-reduce.22.cloned.1.call-done = bf16[1024,1024]{1,0:T(8,128)(2,1)} async-done(((bf16[1024,1024]{1,0:T(8,128)(2,1)}), bf16[1024,1024]{1,0:T(8,128)(2,1)}) %all-reduce.22.cloned.1.call-update) | async-done | bytes 2097168 | tf_op jit(solution)/shard_map/psum | solution.py:55
  219.7 2.5 fusion.50
  222.2 3.0 multiply_reduce_fusion.2
  225.3 28.2 %all-gather.6.cloned.1.call-done = bf16[1024,1024]{1,0:T(8,128)(2,1)} async-done(((bf16[512,1024]{1,0:T(8,128)(2,1)}), bf16[1024,1024]{1,0:T(8,128)(2,1)}) %all-gather.6.cloned.1.call-update) | async-done | bytes 2097168 | tf_op jit(solution)/shard_map/all_gather | solution.py:139
  253.4 7.4 fusion.69
  260.8 27.1 %all-gather.8.cloned.1.call-done = bf16[1024,1024]{1,0:T(8,128)(2,1)} async-done(((bf16[1024,512]{1,0:T(8,128)(2,1)}), bf16[1024,1024]{1,0:T(8,128)(2,1)}) %all-gather.8.cloned.1.call-update) | async-done | bytes 2097168 | tf_op jit(solution)/shard_map/all_gather | solution.py:140
  287.9 16.0 %convert_reduce_fusion.4 = (f32[1024]{0:T(1024)}, bf16[1024,1024]{1,0:T(8,128)(2,1)S(1)}, f32[1024,1024]{1,0:T(8,128)}) fusion(f32[1024,1024]{1,0:T(8,128)} %fusion.69, f32[1024]{0:T(1024)S(1)} %copy-done.50, bf16[1024,1024]{1,0:T(8,128)(2,1)S(1)} %bitcast.274, bf16[1024,1024]{1,0:T(8,128)(2,1)} %all-gather.8.cloned.1.call-done), kind=kOutput, calls=%fused_computation.82 | convolution fusion | flops 2226125824 | bytes 14688256 | tf_op jit(solution)/shard_map/dot_general | solution.py:49
  305.2 3.7 convolution_convert_fusion.2
  308.9 12.1 %reduce-scatter.7.cloned.1.call-start = ((), (), s32[]{:S(2)}) async-start(), calls=%async_computation.14 | async-start | bytes 786432 | tf_op jit(solution)/shard_map/reduce_scatter | solution.py:266
  321.1 74.2 %all-reduce.24.cloned.1.call-done = bf16[1024,1024]{1,0:T(8,128)(2,1)} async-done(((bf16[1024,1024]{1,0:T(8,128)(2,1)}), bf16[1024,1024]{1,0:T(8,128)(2,1)}) %all-reduce.24.cloned.1.call-update) | async-done | bytes 2097168 | tf_op jit(solution)/shard_map/psum | solution.py:55
  395.3 4.5 convert_reduce_fusion.1
  400.0 2.7 fusion.34
  402.7 2.4 fusion.70
  405.0 2.0 copy-done.3
  408.6 4.6 multiply_convert_fusion.1
  414.5 3.8 convolution_convert_fusion
  418.3 3.0 convolution_convert_fusion.6
  422.5 3.5 all-to-all-start.2
  426.0 6.9 convolution_convert_fusion.1
  433.0 1.8 all-to-all-done.2
  436.1 103.6 %while.56 = (s32[]{:T(128)}, bf16[2,2048,64]{2,0,1:T(2,128)(2,1)}, bf16[2,2048,64]{1,2,0:T(8,128)(2,1)}, bf16[2,2048,64]{1,2,0:T(8,128)(2,1)}, bf16[2,2048,64]{2...) while((s32[]{:T(128)}, bf16[2,2048,64]{2,0,1:T(2,128)(2,1)}, ...), condition=%wide.region_19.20_spmd, body=%wide.region_15.19_spmd.sunk | while | flops 680164864 | bytes 41838996 | solution.py:217
  440.5 20.1 %while.58 = (s32[]{:T(128)}, f32[2048,64]{0,1:T(8,128)S(1)}, f32[2048,64]{0,1:T(8,128)S(1)}, f32[4,512,64]{1,2,0:T(8,128)}, bf16[4,512,64]{2,1,0:T(8,128)(2,1)S(...) while((s32[]{:T(128)}, f32[2048,64]{0,1:T(8,128)S(1)}, ...), condition=%wide.region_18.18_spmd.clone, body=%wide.region_16.17_spmd.clone.sunk | while | flops 680164864 | bytes 35530900 | solution.py:111
  462.0 25.1 %dynamic_update_slice.47 = bf16[2,2048,64]{2,0,1:T(2,128)(2,1)} dynamic-update-slice(bf16[2,2048,64]{2,0,1:T(2,128)(2,1)} %get-tuple-element.795, f32[1,2048,64]{2,0,1:T(1,128)S(1)} %bitcast.268, s32[]{:T(128)S(6)} %copy.189, s32[]{:T(128)} %constant.78.clone.1..sunk.2, s32[]{:T(128)} %constant.78.clone.1..sunk.2) | dynamic-update-slice | bytes 1048580 | tf_op jit(solution)/shard_map/while/body/jit(dynamic_update_index_in_dim)/dynamic_update_slice | solution.py:217
  492.3 20.1 %while.58 = (s32[]{:T(128)}, f32[2048,64]{0,1:T(8,128)S(1)}, f32[2048,64]{0,1:T(8,128)S(1)}, f32[4,512,64]{1,2,0:T(8,128)}, bf16[4,512,64]{2,1,0:T(8,128)(2,1)S(...) while((s32[]{:T(128)}, f32[2048,64]{0,1:T(8,128)S(1)}, ...), condition=%wide.region_18.18_spmd.clone, body=%wide.region_16.17_spmd.clone.sunk | while | flops 680164864 | bytes 35530900 | solution.py:111
  513.8 25.1 %dynamic_update_slice.47 = bf16[2,2048,64]{2,0,1:T(2,128)(2,1)} dynamic-update-slice(bf16[2,2048,64]{2,0,1:T(2,128)(2,1)} %get-tuple-element.795, f32[1,2048,64]{2,0,1:T(1,128)S(1)} %bitcast.268, s32[]{:T(128)S(6)} %copy.189, s32[]{:T(128)} %constant.78.clone.1..sunk.2, s32[]{:T(128)} %constant.78.clone.1..sunk.2) | dynamic-update-slice | bytes 1048580 | tf_op jit(solution)/shard_map/while/body/jit(dynamic_update_index_in_dim)/dynamic_update_slice | solution.py:217
  539.7 3.6 copy.142
  543.3 3.6 copy.141
  546.8 7.2 fusion.79
  554.0 3.3 reshape.228
  557.3 24.7 %all_to_all.57 = bf16[4,2,98304]{2,1,0:T(2,128)(2,1)} all-to-all(bf16[4,2,98304]{2,1,0:T(2,128)(2,1)} %reshape.228), channel_id=1, replica_groups=mesh['fsdp'=2,'ctx'=4,'tp'=4] {'ctx'}, dimensions={0} | all-to-all | bytes 3145728 | tf_op jit(solution)/shard_map/all_to_all | solution.py:227
  582.0 3.8 reshape.229
  585.8 6.4 copy.92
  601.3 4.9 fusion.61
  606.3 5.4 convolution_convert_fusion.3
  611.7 3.1 bitcast_convert_fusion
  615.2 2.1 convert_reduce_fusion.3
  618.7 11.9 %reduce-scatter.5.cloned.1.call-done = bf16[3,512,256]{1,2,0:T(8,128)(2,1)} async-done(((bf16[3,1024,256]{1,2,0:T(8,128)(2,1)}), bf16[3,512,256]{1,2,0:T(8,128)(2,1)}) %reduce-scatter.5.cloned.1.call-update) | async-done | bytes 786448 | tf_op jit(solution)/shard_map/reduce_scatter | solution.py:263
  630.7 157.9 %all-reduce.26.cloned.1.call-done = (bf16[1024,1024]{1,0:T(8,128)(2,1)}, bf16[1024,1024]{1,0:T(8,128)(2,1)}) async-done(((bf16[1024,1024]{1,0:T(8,128)(2,1)}, bf16[1024,1024]{1,0:T(8,128)(2,1)}), (bf16[1024,1024]{1,0:T(8,128)(2,1)}, bf16[1024,1024]{1,0:T(8,128)(2,1)})) %all-reduce.26.cloned.1.call-update) | async-done | bytes 4194320 | tf_op jit(solution)/shard_map/psum | solution.py:55
  788.6 3.1 convert_reduce_fusion
  791.7 2.7 fusion.35
  794.5 26.2 %all-reduce.14 = (f32[3,256]{1,0:T(4,128)}, f32[1024]{0:T(1024)}, f32[2,1024]{1,0:T(2,128)}, f32[2,1024]{1,0:T(2,128)}, f32[2,1024]{1,0:T(2,128)}) all-reduce(f32[3,256]{1,0:T(4,128)S(1)} %convert_reduce_fusion.5, f32[1024]{0:T(1024)S(1)} %copy-done.52, ...), channel_id=1, replica_groups=mesh['fsdp'=2,'ctx'=4,'tp'=4] {'fsdp','ctx'}, use_global_device_ids=true, to_apply=%region_26.27 | all-reduce | flops 7936 | bytes 63488 | tf_op jit(solution)/shard_map/psum | solution.py:282
  820.7 7.1 add_add_fusion.2
  827.9 31.4 %all-reduce.28.cloned.1.call-done = (bf16[3,512,256]{1,2,0:T(8,128)(2,1)}, bf16[256,512]{1,0:T(8,128)(2,1)}, bf16[512,1024]{1,0:T(8,128)(2,1)}, bf16[1024,512]{1,0:T(8,128)(2,1)}) async-done(((bf16[3,512,256]{1,2,0:T(8,128)(2,1)}, bf16[256,512]{1,0:T(8,128)(2,1)}, bf16[512,1024]{1,0:T(8,128)(2,1)}, bf16[1024,512]{1,0:T(8,128)(2,1)}), (bf16[3,512,256]{1,2,0:T(8,128)(2,1)}, bf16[256,512]{1,0:T(8,128)(2,1)}, ...) | async-done | bytes 3145744 | tf_op jit(solution)/shard_map/psum | solution.py:277
  859.2 1.9 convert_element_type.168
  861.1 2.5 copy.98
  863.7 2.8 convert_element_type.170
  (335 shorter events, 116.5 us)
Async XLA Ops:
  7.2 4.5 copy-start
  7.2 5.3 copy-start.46
  7.2 5.8 copy-start.47
  7.2 6.4 copy-start.48
  7.2 32.9 %all-gather.4.cloned.1.call-start = ((), (), s32[]{:S(2)}) async-start(), calls=%async_computation.8 | async-start | bytes 2359296 | tf_op jit(solution)/shard_map/all_gather | solution.py:137
  11.7 28.4 %copy-start.55 = (f32[3,256]{1,0:T(4,128)S(1)}, f32[3,256]{1,0:T(4,128)}, u32[]{:S(2)}) copy-start(f32[3,256]{1,0:T(4,128)} %param.23) | copy-start | bytes 9220
  11.7 3.4 copy-start.31
  12.5 2.6 copy-start.38
  15.0 30.8 %copy-start.15 = (f32[1024,10]{0,1:T(8,128)}, f32[1024,10]{0,1:T(8,128)S(1)}, u32[]{:S(2)}) copy-start(f32[1024,10]{0,1:T(8,128)S(1)} %get-tuple-element.436) | copy-start | bytes 122884
  15.0 30.8 %copy-start.17 = (f32[1024,10]{0,1:T(8,128)}, f32[1024,10]{0,1:T(8,128)S(1)}, u32[]{:S(2)}) copy-start(f32[1024,10]{0,1:T(8,128)S(1)} %get-tuple-element.437) | copy-start | bytes 122884
  15.0 30.8 %copy-start.19 = (f32[1024,10]{0,1:T(8,128)}, f32[1024,10]{0,1:T(8,128)S(1)}, u32[]{:S(2)}) copy-start(f32[1024,10]{0,1:T(8,128)S(1)} %get-tuple-element.438) | copy-start | bytes 122884
  15.1 30.8 %copy-start.21 = (f32[1024,10]{0,1:T(8,128)}, f32[1024,10]{0,1:T(8,128)S(1)}, u32[]{:S(2)}) copy-start(f32[1024,10]{0,1:T(8,128)S(1)} %get-tuple-element.449) | copy-start | bytes 122884
  15.1 30.8 %copy-start.23 = (f32[1024,10]{0,1:T(8,128)}, f32[1024,10]{0,1:T(8,128)S(1)}, u32[]{:S(2)}) copy-start(f32[1024,10]{0,1:T(8,128)S(1)} %get-tuple-element.450) | copy-start | bytes 122884
  15.1 30.8 %copy-start.25 = (f32[1024,10]{0,1:T(8,128)}, f32[1024,10]{0,1:T(8,128)S(1)}, u32[]{:S(2)}) copy-start(f32[1024,10]{0,1:T(8,128)S(1)} %get-tuple-element.451) | copy-start | bytes 122884
  54.5 23.8 %all-to-all-start = ((bf16[3,2,512,256]{2,1,0,3:T(2,128)(2,1)}), bf16[3,2,512,256]{2,1,0,3:T(2,128)(2,1)S(1)}, u32[]{:S(2)}, u32[]{:S(2)}) async-start(bf16[3,2,512,256]{2,1,0,3:T(2,128)(2,1)} %pad_maximum_fusion.1), calls=%async_computation | async-start | bytes 3145728 | tf_op jit(solution)/shard_map/all_to_all | solution.py:161
  84.4 11.4 %copy-start.28 = (bf16[2,4,512,64]{2,3,1,0:T(8,128)(2,1)S(1)}, bf16[2,4,512,64]{2,3,1,0:T(8,128)(2,1)}, u32[]{:S(2)}) copy-start(bf16[2,4,512,64]{2,3,1,0:T(8,128)(2,1)} %get-tuple-element.762) | copy-start | bytes 1572868 | tf_op jit(solution)/shard_map/while
  98.0 11.4 %copy-start.28 = (bf16[2,4,512,64]{2,3,1,0:T(8,128)(2,1)S(1)}, bf16[2,4,512,64]{2,3,1,0:T(8,128)(2,1)}, u32[]{:S(2)}) copy-start(bf16[2,4,512,64]{2,3,1,0:T(8,128)(2,1)} %get-tuple-element.762) | copy-start | bytes 1572868 | tf_op jit(solution)/shard_map/while
  110.2 19.6 %copy-start.5 = (bf16[2,2048,64]{2,1,0:T(8,128)(2,1)}, bf16[2,2048,64]{2,1,0:T(8,128)(2,1)S(1)}, u32[]{:S(2)}) copy-start(bf16[2,2048,64]{2,1,0:T(8,128)(2,1)S(1)} %get-tuple-element.841) | copy-start | bytes 1572868
  110.3 7.7 copy-start.30
  114.4 12.8 %all-to-all-start.1 = ((bf16[4,2,32768]{2,1,0:T(2,128)(2,1)}), bf16[4,2,32768]{2,1,0:T(2,128)(2,1)S(1)}, u32[]{:S(2)}, u32[]{:S(2)}) async-start(bf16[4,2,32768]{2,1,0:T(2,128)(2,1)} %reshape.226), calls=%async_computation.1 | async-start | bytes 1048576 | tf_op jit(solution)/shard_map/all_to_all | solution.py:174
  117.9 101.8 %all-reduce.22.cloned.1.call-start = ((), (), s32[]{:S(2)}) async-start(), calls=%async_computation.9 | async-start | bytes 4194304 | tf_op jit(solution)/shard_map/psum | solution.py:55
  129.9 5.0 copy-start.49
  129.9 89.8 %copy-start.1 = (bf16[2,512,1024]{2,1,0:T(8,128)(2,1)S(1)}, bf16[2,512,1024]{2,1,0:T(8,128)(2,1)}, u32[]{:S(2)}) copy-start(bf16[2,512,1024]{2,1,0:T(8,128)(2,1)} %param.20) | copy-start | bytes 6291460
  133.2 120.2 %all-gather.6.cloned.1.call-start = ((), (), s32[]{:S(2)}) async-start(), calls=%async_computation.10 | async-start | bytes 3145728 | tf_op jit(solution)/shard_map/all_gather | solution.py:139
  134.0 154.0 %all-gather.8.cloned.1.call-start = ((), (), s32[]{:S(2)}) async-start(), calls=%async_computation.11 | async-start | bytes 3145728 | tf_op jit(solution)/shard_map/all_gather | solution.py:140
  134.5 260.7 %all-reduce.24.cloned.1.call-start = ((), (), s32[]{:S(2)}) async-start(), calls=%async_computation.12 | async-start | bytes 4194304 | tf_op jit(solution)/shard_map/psum | solution.py:55
  135.5 89.7 %copy-start.36 = (f32[1,1024]{1,0:T(1,128)}, f32[1,1024]{1,0:T(1,128)S(1)}, u32[]{:S(2)}) copy-start(f32[1,1024]{1,0:T(1,128)S(1)} %get-tuple-element.442) | copy-start | bytes 12292
  219.7 2.5 copy-start.6
  222.2 31.2 %copy-start.35 = (f32[1,1024]{1,0:T(1,128)S(1)}, f32[1,1024]{1,0:T(1,128)}, u32[]{:S(2)}) copy-start(f32[1,1024]{1,0:T(1,128)} %get-tuple-element.443) | copy-start | bytes 12292
  222.2 31.2 %copy-start.51 = (f32[1,1024]{1,0:T(1,128)S(1)}, f32[1,1024]{1,0:T(1,128)}, u32[]{:S(2)}) copy-start(f32[1,1024]{1,0:T(1,128)} %get-tuple-element.445) | copy-start | bytes 12292
  253.4 34.5 %copy-start.10 = (bf16[2,512,1024]{2,1,0:T(8,128)(2,1)S(1)}, bf16[2,512,1024]{2,1,0:T(8,128)(2,1)}, u32[]{:S(2)}) copy-start(bf16[2,512,1024]{2,1,0:T(8,128)(2,1)} %param.31) | copy-start | bytes 6291460
  253.4 34.5 %copy-start.50 = (f32[1024]{0:T(1024)S(1)}, f32[1024]{0:T(1024)}, u32[]{:S(2)}) copy-start(f32[1024]{0:T(1024)} %param.26) | copy-start | bytes 12292
  287.9 17.3 %copy-start.53 = (bf16[1024,1024]{1,0:T(8,128)(2,1)S(1)}, bf16[1024,1024]{1,0:T(8,128)(2,1)}, u32[]{:S(2)}) copy-start(bf16[1024,1024]{1,0:T(8,128)(2,1)} %all-gather.6.cloned.1.call-done) | copy-start | bytes 6291460
  308.9 309.7 %reduce-scatter.7.cloned.1.call-start = ((), (), s32[]{:S(2)}) async-start(), calls=%async_computation.14 | async-start | bytes 786432 | tf_op jit(solution)/shard_map/reduce_scatter | solution.py:266
  395.2 4.5 copy-start.4
  395.3 4.7 copy-start.7
  405.0 2.0 copy-start.3
  408.5 210.2 %reduce-scatter.11.cloned.1.call-start = ((), (), s32[]{:S(2)}) async-start(), calls=%async_computation.16 | async-start | bytes 3145728 | tf_op jit(solution)/shard_map/reduce_scatter | solution.py:272
  422.5 12.3 %all-to-all-start.2 = ((bf16[2,512,256]{1,0,2:T(2,128)(2,1)}), bf16[2,512,256]{1,0,2:T(2,128)(2,1)S(1)}, u32[]{:S(2)}, u32[]{:S(2)}) async-start(bf16[2,512,256]{1,0,2:T(2,128)(2,1)} %copy.83), calls=%async_computation.2 | async-start | bytes 1048576 | tf_op jit(solution)/shard_map/all_to_all | solution.py:211
  426.0 192.7 %reduce-scatter.9.cloned.1.call-start = ((), (), s32[]{:S(2)}) async-start(), calls=%async_computation.15 | async-start | bytes 3145728 | tf_op jit(solution)/shard_map/reduce_scatter | solution.py:269
  432.9 197.7 %reduce-scatter.5.cloned.1.call-start = ((), (), s32[]{:S(2)}) async-start(), calls=%async_computation.13 | async-start | bytes 2359296 | tf_op jit(solution)/shard_map/reduce_scatter | solution.py:263
  592.2 2.9 copy-start.9
  596.4 1.7 copy-start.16
  596.4 1.7 copy-start.18
  596.4 1.7 copy-start.20
  598.9 2.4 copy-start.13
  601.3 5.0 copy-start.12
  606.2 182.3 %all-reduce.26.cloned.1.call-start = ((), (), s32[]{:S(2)}) async-start(), calls=%async_computation.17 | async-start | bytes 8388608 | tf_op jit(solution)/shard_map/psum | solution.py:55
  606.3 5.4 copy-start.14
  606.3 5.4 copy-start.54
  614.8 2.5 copy-start.42
  614.8 173.7 %copy-start.2 = (bf16[2,512,1024]{2,1,0:T(8,128)(2,1)S(1)}, bf16[2,512,1024]{2,1,0:T(8,128)(2,1)}, u32[]{:S(2)}) copy-start(bf16[2,512,1024]{2,1,0:T(8,128)(2,1)} %param.20) | copy-start | bytes 6291460
  614.8 173.7 %copy-start.32 = (f32[1,4,2,128]{3,1,2,0:T(4,128)S(1)}, f32[1,4,2,128]{3,1,2,0:T(4,128)}, u32[]{:S(2)}) copy-start(f32[1,4,2,128]{3,1,2,0:T(4,128)} %copy-done.31) | copy-start | bytes 12292
  614.9 173.7 %copy-start.34 = (f32[1,1024]{1,0:T(1,128)S(1)}, f32[1,1024]{1,0:T(1,128)}, u32[]{:S(2)}) copy-start(f32[1,1024]{1,0:T(1,128)} %copy-done.33) | copy-start | bytes 12292
  614.9 244.4 %all-reduce.28.cloned.1.call-start = ((), (), s32[]{:S(2)}) async-start(), calls=%async_computation.18 | async-start | bytes 6291456 | tf_op jit(solution)/shard_map/psum | solution.py:277
  617.3 174.4 %copy-start.41 = (f32[1,4,2,128]{3,1,2,0:T(4,128)S(1)}, f32[1,4,2,128]{3,1,2,0:T(4,128)}, u32[]{:S(2)}) copy-start(f32[1,4,2,128]{3,1,2,0:T(4,128)} %copy-done.40) | copy-start | bytes 12292
  617.3 174.4 %copy-start.44 = (f32[1024]{0:T(1024)S(1)}, f32[1024]{0:T(1024)}, u32[]{:S(2)}) copy-start(f32[1024]{0:T(1024)} %get-tuple-element.296) | copy-start | bytes 12292
  617.3 174.4 %copy-start.39 = (f32[1024]{0:T(1024)S(1)}, f32[1024]{0:T(1024)}, u32[]{:S(2)}) copy-start(f32[1024]{0:T(1024)} %copy-done.38) | copy-start | bytes 12292
  788.5 3.2 copy-start.8
  788.5 5.9 copy-start.43
  788.5 5.9 copy-start.52
  788.6 32.2 %copy-start.37 = (f32[1,1024]{1,0:T(1,128)S(1)}, f32[1,1024]{1,0:T(1,128)}, u32[]{:S(2)}) copy-start(f32[1,1024]{1,0:T(1,128)} %copy-done.36) | copy-start | bytes 12292
  788.6 32.2 %copy-start.45 = (f32[1,1024]{1,0:T(1,128)S(1)}, f32[1,1024]{1,0:T(1,128)}, u32[]{:S(2)}) copy-start(f32[1,1024]{1,0:T(1,128)} %get-tuple-element.441) | copy-start | bytes 12292
  859.2 7.2 copy-start.27
  (9 other events, 11.5 us)
Sparse Core Ops, SparseCore 0:
  10.1 29.8 all-gather.3
  133.3 86.3 all-reduce.21
  221.2 32.1 all-gather.5
  254.8 33.0 all-gather.7
  309.1 86.1 all-reduce.23
  408.7 13.6 reduce-scatter.6
  424.6 31.8 reduce-scatter.10
  458.8 31.8 reduce-scatter.8
  606.3 24.2 reduce-scatter.4
  633.5 155.0 all-reduce.25
  791.1 68.0 all-reduce.27
where the time goes:
time: 888 us; the launch traced here: 875 us
  waiting for transfers between devices  461 us (52%)
  local copies, waits for them, and re-layouts  130 us (15%)
  matrix products  113 us (13%)
  other arithmetic  71.1 us (8%)
  blocking collectives  60.2 us (7%)
  starting transfers between devices  23.8 us (3%)
  between operations  15.3 us (2%)
    psum x3, waiting for transfers between devices, tp_whole(): return lax.psum(partial_sum.astype(jnp.bfloat16), 'tp').astype(jnp.float32)  316 us
    dynamic_update_slice x4, local copies, waits for them, and re-layouts, shards(): lax.map(backward_group, (grouped[0], grouped[1], grouped[2], grad_grouped...  51.9 us
    psum x1, waiting for transfers between devices, shards(): lax.psum(shard_qkv.astype(jnp.bfloat16), 'ctx').astype(jnp.float32)  31.4 us
    unnamed x122, local copies, waits for them, and re-layouts  28.2 us
    all_gather x1, waiting for transfers between devices, shards(): lax.all_gather(w_up, 'fsdp', axis=0, tiled=True)  28.2 us
    all_gather x1, waiting for transfers between devices, shards(): lax.all_gather(w_down, 'fsdp', axis=1, tiled=True)  27.1 us
    psum x1, blocking collectives, shards(): lax.psum((norm_vectors[0:2], norm_vectors[2:4], norm_vectors[4:6], grad_b...  26.2 us
    all_to_all x1, blocking collectives, shards(): lax.all_to_all(grad_heads, 'ctx', split_axis=2, concat_axis=3, tiled=True)  24.7 us
  transfers between devices with their start and end apart: 14, of which 10 were waited for; matrix products, arithmetic and copies ran while one was open for 24% of the time, Pallas kernels for 0%

commit v1 on v0

--- a/solution.py
+++ b/solution.py
@@ -9,6 +9,28 @@
 ROT = 20
 QBLK = 512
 EPSILON = 1e-06
+
+
+def laid_out(pieces, dim):
+    pieces = jnp.moveaxis(pieces, 0, dim)
+    shape = pieces.shape
+    return pieces.reshape(*shape[:dim], shape[dim] * shape[dim + 1], *shape[dim + 2 :])
+
+
+def grow_blocks(x, axis):
+    devices = lax.axis_size(axis)
+    blocks = x[None]
+    for level in range(devices.bit_length() - 1):
+        apart = 1 << level
+        other = lax.ppermute(blocks, axis, [(i, i ^ apart) for i in range(devices)])
+        both = jnp.stack([blocks, other])
+        upper = lax.axis_index(axis) >> level & 1
+        blocks = jnp.where(upper == 0, both, both[::-1]).reshape(-1, *x.shape)
+    return blocks
+
+
+def collect(array, axis, dim):
+    return laid_out(grow_blocks(array, axis), dim)
 
 
 def layer_norm(values, gain_vec, shift_vec):
@@ -134,7 +156,7 @@
     group_count = clip_count * group_heads
     inputs = block_input.reshape(row_count, width).astype(jnp.float32)
     full_qkv, full_proj, full_up, full_down = (
-        lax.all_gather(w_qkv, "fsdp", axis=1, tiled=True),
+        collect(w_qkv, "fsdp", 1),
         lax.all_gather(w_proj, "fsdp", axis=1, tiled=True),
         lax.all_gather(w_up, "fsdp", axis=0, tiled=True),
         lax.all_gather(w_down, "fsdp", axis=1, tiled=True),

time: 888 us -> 808 us (0.910)
  waiting for transfers between devices: 461 us -> 415 us
  blocking collectives: 60.2 us -> 35 us
    all_gather x1, waiting for transfers between devices: 28.2 us -> 0.03 us  [shards(): lax.all_gather(w_up, 'fsdp', axis=0, tiled=True)]
    all_gather x1, waiting for transfers between devices: 27.1 us -> 0.01 us  [shards(): lax.all_gather(w_down, 'fsdp', axis=1, tiled=True)]
    all_to_all x1 -> x0, blocking collectives: 24.7 us -> none  [shards(): lax.all_to_all(grad_heads, 'ctx', split_axis=2, concat_axis=3, tiled=True)]
    all_gather x1, waiting for transfers between devices: 22.8 us -> 0.03 us  [shards(): lax.all_gather(w_qkv, 'fsdp', axis=1, tiled=True)]
    reduce_scatter x1, waiting for transfers between devices: 11.9 us -> 25 us  [shards(): lax.psum_scatter(grad_qkv.astype(jnp.bfloat16), 'fsdp', scatter_dimension...]
    reduce_scatter x1, starting transfers between devices: 12.1 us -> 0.04 us  [shards(): lax.psum_scatter(grad_proj.astype(jnp.bfloat16), 'fsdp', scatter_dimensio...]
    all_to_all x0 -> x1, waiting for transfers between devices: none -> 9.55 us  [shards(): lax.all_to_all(grad_heads, 'ctx', split_axis=2, concat_axis=3, tiled=True)]
    ppermute x0 -> x1, waiting for transfers between devices: none -> 9.37 us  [grow_blocks(): other = lax.ppermute(blocks, axis, [(i, i ^ apart) for i in range(devices)])]
  transfers between devices with their start and end apart: 14 -> 16, of which waited for: 10 -> 9; matrix products, arithmetic and copies ran while one was open for 24% -> 11% of each run, Pallas kernels for 0% -> 0%
where the time goes in v1:
time: 808 us; the launch traced here: 794 us
  waiting for transfers between devices  415 us (51%)
  local copies, waits for them, and re-layouts  123 us (15%)
  matrix products  111 us (14%)
  other arithmetic  73.4 us (9%)
  blocking collectives  35 us (4%)
  starting transfers between devices  19.2 us (2%)
  between operations  17 us (2%)
    psum x3, waiting for transfers between devices, tp_whole(): return lax.psum(partial_sum.astype(jnp.bfloat16), 'tp').astype(jnp.float32)  307 us
    dynamic_update_slice x4, local copies, waits for them, and re-layouts, shards(): lax.map(backward_group, (grouped[0], grouped[1], grouped[2], grad_grouped...  51.9 us
    psum x1, waiting for transfers between devices, shards(): lax.psum(shard_qkv.astype(jnp.bfloat16), 'ctx').astype(jnp.float32)  33.1 us
    unnamed x139, local copies, waits for them, and re-layouts  25.9 us
    psum x1, blocking collectives, shards(): lax.psum((norm_vectors[0:2], norm_vectors[2:4], norm_vectors[4:6], grad_b...  25.7 us
    dot_general x19, matrix products, contract_rows(): lax.dot_general(left_mat, right_mat, (((0,), (0,)), ((), ())), preferred_...  25.1 us
    reduce_scatter x1, waiting for transfers between devices, shards(): lax.psum_scatter(grad_qkv.astype(jnp.bfloat16), 'fsdp', scatter_dimension...  25 us
    dot_general x3, matrix products, contract_cols(): lax.dot_general(left_mat, right_mat, (((1,), (1,)), ((), ())), preferred_...  20.8 us
  transfers between devices with their start and end apart: 16, of which 9 were waited for; matrix products, arithmetic and copies ran while one was open for 11% of the time, Pallas kernels for 0%

profile of v1, /device:TPU:0, one launch (start us, length us, event | category | flops | bytes accessed | tf_op | source)
XLA Modules:
  0.0 794.1 jit_solution(12692247597143020800)
XLA Ops:
  8.1 3.1 collective-permute-start
  11.1 1.9 convert_reduce_fusion.2
  13.7 2.3 fusion.43
  19.5 9.4 %collective-permute-done = bf16[1,3,512,256]{3,2,1,0:T(8,128)(2,1)S(1)} collective-permute-done((bf16[1,3,512,256]{3,2,1,0:T(8,128)(2,1)}, bf16[1,3,512,256]{3,2,1,0:T(8,128)(2,1)S(1)}, u32[]{:S(2)}, u32[]{:S(2)}) %collective-permute-start) | collective-permute-done | bytes 786464 | tf_op jit(solution)/shard_map/ppermute | solution.py:25
  29.4 1.9 add_bitcast_fusion
  36.1 3.1 pad_maximum_fusion.2
  39.2 3.8 all-to-all-start
  43.0 20.0 %all-to-all-done = bf16[3,2,512,256]{2,1,0,3:T(2,128)(2,1)S(1)} async-done(((bf16[3,2,512,256]{2,1,0,3:T(2,128)(2,1)}), bf16[3,2,512,256]{2,1,0,3:T(2,128)(2,1)S(1)}, u32[]{:S(2)}, u32[]{:S(2)}) %all-to-all-start) | async-done | bytes 1572896 | tf_op jit(solution)/shard_map/all_to_all | solution.py:183
  67.6 27.2 %while.54 = (s32[]{:T(128)}, bf16[2,4,512,64]{2,3,1,0:T(8,128)(2,1)}, f32[2,4,512]{2,1,0:T(4,128)S(1)}, bf16[2,2048,64]{2,1,0:T(8,128)(2,1)S(1)}, bf16[2,2048,64...) while((s32[]{:T(128)}, ...), condition=%wide.region_7.8_spmd, body=%wide.region_2.7_spmd.sunk | while | flops 277904896 | bytes 20156772 | solution.py:190
  69.0 11.4 %while.57 = (s32[]{:T(128)}, bf16[4,512,64]{1,2,0:T(8,128)(2,1)S(1)}, f32[4,512]{1,0:T(4,128)S(1)}, bf16[4,512,64]{2,1,0:T(8,128)(2,1)S(1)}, bf16[2048,64]{1,0:T...) while((s32[]{:T(128)}, bf16[4,512,64]{1,2,0:T(8,128)(2,1)S(1)}, ...), condition=%wide.region_6.6_spmd, body=%wide.region_3.5_spmd.sunk | while | flops 277904896 | bytes 13848681 | solution.py:98
  82.6 11.4 %while.57 = (s32[]{:T(128)}, bf16[4,512,64]{1,2,0:T(8,128)(2,1)S(1)}, f32[4,512]{1,0:T(4,128)S(1)}, bf16[4,512,64]{2,1,0:T(8,128)(2,1)S(1)}, bf16[2048,64]{1,0:T...) while((s32[]{:T(128)}, bf16[4,512,64]{1,2,0:T(8,128)(2,1)S(1)}, ...), condition=%wide.region_6.6_spmd, body=%wide.region_3.5_spmd.sunk | while | flops 277904896 | bytes 13848681 | solution.py:98
  94.8 2.6 copy.96
  97.4 1.6 reshape.256
  99.0 3.5 all-to-all-start.1
  102.5 9.3 %all_gather.15 = bf16[256,1024]{1,0:T(8,128)(2,1)S(1)} all-gather(bf16[256,512]{1,0:T(8,128)(2,1)S(1)} %copy-done.36), channel_id=1, replica_groups=mesh['fsdp'=2,'ctx'=4,'tp'=4] {'fsdp'}, dimensions={1}, use_global_device_ids=true | all-gather | bytes 786432 | tf_op jit(solution)/shard_map/all_gather | solution.py:160
  114.3 2.1 convolution_convert_fusion.4
  118.2 86.1 %all-reduce.22.cloned.1.call-done = bf16[1024,1024]{1,0:T(8,128)(2,1)} async-done(((bf16[1024,1024]{1,0:T(8,128)(2,1)}), bf16[1024,1024]{1,0:T(8,128)(2,1)}) %all-reduce.22.cloned.1.call-update) | async-done | bytes 2097168 | tf_op jit(solution)/shard_map/psum | solution.py:77
  204.3 2.5 fusion.54
  206.8 3.0 multiply_reduce_fusion.2
  209.9 7.4 fusion.71
  217.3 16.4 %convert_reduce_fusion.4 = (f32[1024]{0:T(1024)}, bf16[1024,1024]{1,0:T(8,128)(2,1)S(1)}, f32[1024,1024]{1,0:T(8,128)}) fusion(f32[1024,1024]{1,0:T(8,128)} %fusion.71, f32[1024]{0:T(1024)S(1)} %copy-done.57, bf16[1024,1024]{1,0:T(8,128)(2,1)S(1)} %bitcast.282, bf16[1024,1024]{1,0:T(8,128)(2,1)} %all-gather.6.cloned.1.call-done), kind=kOutput, calls=%fused_computation.86 | convolution fusion | flops 2226125824 | bytes 14688256 | tf_op jit(solution)/shard_map/dot_general | solution.py:71
  235.0 3.7 convolution_convert_fusion.2
  238.7 85.3 %all-reduce.24.cloned.1.call-done = bf16[1024,1024]{1,0:T(8,128)(2,1)} async-done(((bf16[1024,1024]{1,0:T(8,128)(2,1)}), bf16[1024,1024]{1,0:T(8,128)(2,1)}) %all-reduce.24.cloned.1.call-update) | async-done | bytes 2097168 | tf_op jit(solution)/shard_map/psum | solution.py:77
  324.1 4.5 convert_reduce_fusion.1
  328.8 2.7 fusion.34
  331.5 2.4 fusion.72
  333.9 2.0 copy-done.3
  337.8 3.6 all-to-all-start.2
  341.5 8.8 %all-to-all-done.2 = bf16[2,512,256]{1,0,2:T(2,128)(2,1)S(1)} async-done(((bf16[2,512,256]{1,0,2:T(2,128)(2,1)}), bf16[2,512,256]{1,0,2:T(2,128)(2,1)S(1)}, u32[]{:S(2)}, u32[]{:S(2)}) %all-to-all-start.2) | async-done | bytes 524320 | tf_op jit(solution)/shard_map/all_to_all | solution.py:233
  351.6 103.6 %while.56 = (s32[]{:T(128)}, bf16[2,2048,64]{2,0,1:T(2,128)(2,1)}, bf16[2,2048,64]{1,2,0:T(8,128)(2,1)}, bf16[2,2048,64]{1,2,0:T(8,128)(2,1)}, bf16[2,2048,64]{2...) while((s32[]{:T(128)}, bf16[2,2048,64]{2,0,1:T(2,128)(2,1)}, ...), condition=%wide.region_19.20_spmd, body=%wide.region_15.19_spmd.sunk | while | flops 680164864 | bytes 41838996 | solution.py:239
  356.0 20.1 %while.58 = (s32[]{:T(128)}, f32[2048,64]{0,1:T(8,128)S(1)}, f32[2048,64]{0,1:T(8,128)S(1)}, f32[4,512,64]{1,2,0:T(8,128)}, bf16[4,512,64]{2,1,0:T(8,128)(2,1)S(...) while((s32[]{:T(128)}, f32[2048,64]{0,1:T(8,128)S(1)}, ...), condition=%wide.region_18.18_spmd.clone, body=%wide.region_16.17_spmd.clone.sunk | while | flops 680164864 | bytes 35530900 | solution.py:133
  374.6 1.5 fusion.133
  377.5 25.1 %dynamic_update_slice.47 = bf16[2,2048,64]{2,0,1:T(2,128)(2,1)} dynamic-update-slice(bf16[2,2048,64]{2,0,1:T(2,128)(2,1)} %get-tuple-element.800, f32[1,2048,64]{2,0,1:T(1,128)S(1)} %bitcast.276, s32[]{:T(128)S(6)} %copy.184, s32[]{:T(128)} %constant.81.clone.1..sunk.2, s32[]{:T(128)} %constant.81.clone.1..sunk.2) | dynamic-update-slice | bytes 1048580 | tf_op jit(solution)/shard_map/while/body/jit(dynamic_update_index_in_dim)/dynamic_update_slice | solution.py:239
  407.8 20.1 %while.58 = (s32[]{:T(128)}, f32[2048,64]{0,1:T(8,128)S(1)}, f32[2048,64]{0,1:T(8,128)S(1)}, f32[4,512,64]{1,2,0:T(8,128)}, bf16[4,512,64]{2,1,0:T(8,128)(2,1)S(...) while((s32[]{:T(128)}, f32[2048,64]{0,1:T(8,128)S(1)}, ...), condition=%wide.region_18.18_spmd.clone, body=%wide.region_16.17_spmd.clone.sunk | while | flops 680164864 | bytes 35530900 | solution.py:133
  426.4 1.5 fusion.133
  429.2 25.1 %dynamic_update_slice.47 = bf16[2,2048,64]{2,0,1:T(2,128)(2,1)} dynamic-update-slice(bf16[2,2048,64]{2,0,1:T(2,128)(2,1)} %get-tuple-element.800, f32[1,2048,64]{2,0,1:T(1,128)S(1)} %bitcast.276, s32[]{:T(128)S(6)} %copy.184, s32[]{:T(128)} %constant.81.clone.1..sunk.2, s32[]{:T(128)} %constant.81.clone.1..sunk.2) | dynamic-update-slice | bytes 1048580 | tf_op jit(solution)/shard_map/while/body/jit(dynamic_update_index_in_dim)/dynamic_update_slice | solution.py:239
  455.2 3.6 copy.137
  458.8 3.6 copy.136
  462.3 7.2 fusion.81
  469.5 3.3 reshape.258
  472.8 4.3 all-to-all-start.3
  478.0 4.7 multiply_convert_fusion.1
  484.1 3.7 convolution_convert_fusion.3
  487.7 9.6 %all-to-all-done.3 = bf16[4,2,98304]{2,1,0:T(2,128)(2,1)} async-done(((bf16[4,2,98304]{2,1,0:T(2,128)(2,1)}), bf16[4,2,98304]{2,1,0:T(2,128)(2,1)}, u32[]{:S(2)}, u32[]{:S(2)}) %all-to-all-start.3) | async-done | bytes 1572896 | tf_op jit(solution)/shard_map/all_to_all | solution.py:249
  497.3 3.8 reshape.259
  501.0 6.4 copy.88
  507.5 1.5 slice.204
  515.8 4.7 bitcast_convert_fusion
  521.6 3.7 convolution_convert_fusion.5
  525.6 5.4 convolution_convert_fusion
  531.2 6.9 convolution_convert_fusion.1
  538.2 135.6 %all-reduce.26.cloned.1.call-done = (bf16[1024,1024]{1,0:T(8,128)(2,1)}, bf16[1024,1024]{1,0:T(8,128)(2,1)}) async-done(((bf16[1024,1024]{1,0:T(8,128)(2,1)}, bf16[1024,1024]{1,0:T(8,128)(2,1)}), (bf16[1024,1024]{1,0:T(8,128)(2,1)}, bf16[1024,1024]{1,0:T(8,128)(2,1)})) %all-reduce.26.cloned.1.call-update) | async-done | bytes 4194320 | tf_op jit(solution)/shard_map/psum | solution.py:77
  673.9 3.1 convert_reduce_fusion
  677.0 3.1 fusion.35
  680.1 3.0 fusion.61
  683.3 25.0 %reduce-scatter.5.cloned.1.call-done = bf16[3,512,256]{1,2,0:T(8,128)(2,1)} async-done(((bf16[3,1024,256]{1,2,0:T(8,128)(2,1)}), bf16[3,512,256]{1,2,0:T(8,128)(2,1)}) %reduce-scatter.5.cloned.1.call-update) | async-done | bytes 786448 | tf_op jit(solution)/shard_map/reduce_scatter | solution.py:285
  708.4 2.0 convert_reduce_fusion.3
  711.7 25.7 %all-reduce.14 = (f32[3,256]{1,0:T(4,128)}, f32[1024]{0:T(1024)}, f32[2,1024]{1,0:T(2,128)}, f32[2,1024]{1,0:T(2,128)}, f32[2,1024]{1,0:T(2,128)}) all-reduce(f32[3,256]{1,0:T(4,128)S(1)} %convert_reduce_fusion.5, f32[1024]{0:T(1024)S(1)} %copy-done.61, ...), channel_id=1, replica_groups=mesh['fsdp'=2,'ctx'=4,'tp'=4] {'fsdp','ctx'}, use_global_device_ids=true, to_apply=%region_26.27 | all-reduce | flops 7936 | bytes 63488 | tf_op jit(solution)/shard_map/psum | solution.py:304
  737.4 7.1 add_add_fusion.2
  744.6 33.1 %all-reduce.28.cloned.1.call-done = (bf16[3,512,256]{1,2,0:T(8,128)(2,1)}, bf16[256,512]{1,0:T(8,128)(2,1)}, bf16[512,1024]{1,0:T(8,128)(2,1)}, bf16[1024,512]{1,0:T(8,128)(2,1)}) async-done(((bf16[3,512,256]{1,2,0:T(8,128)(2,1)}, bf16[256,512]{1,0:T(8,128)(2,1)}, bf16[512,1024]{1,0:T(8,128)(2,1)}, bf16[1024,512]{1,0:T(8,128)(2,1)}), (bf16[3,512,256]{1,2,0:T(8,128)(2,1)}, bf16[256,512]{1,0:T(8,128)(2,1)}, ...) | async-done | bytes 3145744 | tf_op jit(solution)/shard_map/psum | solution.py:299
  777.6 1.9 convert_element_type.176
  779.5 2.5 copy.93
  782.1 2.8 convert_element_type.178
  784.9 1.6 convert_element_type.181
  (356 shorter events, 111.8 us)
Async XLA Ops:
  8.0 10.6 %copy-start = (bf16[2,512,1024]{2,1,0:T(8,128)(2,1)S(1)}, bf16[2,512,1024]{2,1,0:T(8,128)(2,1)}, u32[]{:S(2)}) copy-start(bf16[2,512,1024]{2,1,0:T(8,128)(2,1)} %param.20) | copy-start | bytes 6291460
  8.0 7.9 copy-start.54
  8.0 8.5 %copy-start.55 = (f32[2,1024]{1,0:T(2,128)S(1)}, f32[2,1024]{1,0:T(2,128)}, u32[]{:S(2)}) copy-start(f32[2,1024]{1,0:T(2,128)} %param.29) | copy-start | bytes 24580
  8.0 9.1 %copy-start.53 = (s32[3,2,512]{2,1,0:T(2,128)S(1)}, s32[3,2,512]{2,1,0:T(2,128)}, u32[]{:S(2)}) copy-start(s32[3,2,512]{2,1,0:T(2,128)} %param.21) | copy-start | bytes 36868
  8.1 20.8 %collective-permute-start = (bf16[1,3,512,256]{3,2,1,0:T(8,128)(2,1)}, bf16[1,3,512,256]{3,2,1,0:T(8,128)(2,1)S(1)}, u32[]{:S(2)}, u32[]{:S(2)}) collective-permute-start(bf16[1,3,512,256]{3,2,1,0:T(8,128)(2,1)} %bitcast.298), channel_id=1, source_target_pairs={{0,16},{16,0},{1,17},{17,1},{2,18},{18,2},{3,19},{19,3},{4,20},{20... | collective-permute-start | bytes 2359304 | tf_op jit(solution)/shard_map/ppermute | solution.py:25
  13.1 15.8 %copy-start.14 = (bf16[3,512,256]{2,1,0:T(8,128)(2,1)S(1)}, bf16[3,512,256]{2,1,0:T(8,128)(2,1)}, u32[]{:S(2)}) copy-start(bf16[3,512,256]{2,1,0:T(8,128)(2,1)} %param.22) | copy-start | bytes 2359300
  16.6 12.5 %copy-start.37 = (f32[1,1024]{1,0:T(1,128)}, f32[1,1024]{1,0:T(1,128)S(1)}, u32[]{:S(2)}) copy-start(f32[1,1024]{1,0:T(1,128)S(1)} %get-tuple-element.445) | copy-start | bytes 12292
  17.2 11.9 %copy-start.45 = (f32[1,1024]{1,0:T(1,128)}, f32[1,1024]{1,0:T(1,128)S(1)}, u32[]{:S(2)}) copy-start(f32[1,1024]{1,0:T(1,128)S(1)} %get-tuple-element.447) | copy-start | bytes 12292
  18.6 13.4 %copy-start.21 = (f32[1024,10]{0,1:T(8,128)}, f32[1024,10]{0,1:T(8,128)S(1)}, u32[]{:S(2)}) copy-start(f32[1024,10]{0,1:T(8,128)S(1)} %get-tuple-element.437) | copy-start | bytes 122884
  18.6 13.4 %copy-start.23 = (f32[1024,10]{0,1:T(8,128)}, f32[1024,10]{0,1:T(8,128)S(1)}, u32[]{:S(2)}) copy-start(f32[1024,10]{0,1:T(8,128)S(1)} %get-tuple-element.438) | copy-start | bytes 122884
  18.6 13.4 %copy-start.25 = (f32[1024,10]{0,1:T(8,128)}, f32[1024,10]{0,1:T(8,128)S(1)}, u32[]{:S(2)}) copy-start(f32[1024,10]{0,1:T(8,128)S(1)} %get-tuple-element.439) | copy-start | bytes 122884
  18.6 13.4 %copy-start.27 = (f32[1024,10]{0,1:T(8,128)}, f32[1024,10]{0,1:T(8,128)S(1)}, u32[]{:S(2)}) copy-start(f32[1024,10]{0,1:T(8,128)S(1)} %get-tuple-element.454) | copy-start | bytes 122884
  18.6 13.4 %copy-start.29 = (f32[1024,10]{0,1:T(8,128)}, f32[1024,10]{0,1:T(8,128)S(1)}, u32[]{:S(2)}) copy-start(f32[1024,10]{0,1:T(8,128)S(1)} %get-tuple-element.455) | copy-start | bytes 122884
  18.6 13.4 %copy-start.31 = (f32[1024,10]{0,1:T(8,128)}, f32[1024,10]{0,1:T(8,128)S(1)}, u32[]{:S(2)}) copy-start(f32[1024,10]{0,1:T(8,128)S(1)} %get-tuple-element.456) | copy-start | bytes 122884
  19.5 9.9 %copy-start.64 = (f32[3,256]{1,0:T(4,128)S(1)}, f32[3,256]{1,0:T(4,128)}, u32[]{:S(2)}) copy-start(f32[3,256]{1,0:T(4,128)} %param.23) | copy-start | bytes 9220
  39.2 23.8 %all-to-all-start = ((bf16[3,2,512,256]{2,1,0,3:T(2,128)(2,1)}), bf16[3,2,512,256]{2,1,0,3:T(2,128)(2,1)S(1)}, u32[]{:S(2)}, u32[]{:S(2)}) async-start(bf16[3,2,512,256]{2,1,0,3:T(2,128)(2,1)} %pad_maximum_fusion.2), calls=%async_computation | async-start | bytes 3145728 | tf_op jit(solution)/shard_map/all_to_all | solution.py:183
  69.0 11.4 %copy-start.34 = (bf16[2,4,512,64]{2,3,1,0:T(8,128)(2,1)S(1)}, bf16[2,4,512,64]{2,3,1,0:T(8,128)(2,1)}, u32[]{:S(2)}) copy-start(bf16[2,4,512,64]{2,3,1,0:T(8,128)(2,1)} %get-tuple-element.767) | copy-start | bytes 1572868 | tf_op jit(solution)/shard_map/while
  82.6 11.4 %copy-start.34 = (bf16[2,4,512,64]{2,3,1,0:T(8,128)(2,1)S(1)}, bf16[2,4,512,64]{2,3,1,0:T(8,128)(2,1)}, u32[]{:S(2)}) copy-start(bf16[2,4,512,64]{2,3,1,0:T(8,128)(2,1)} %get-tuple-element.767) | copy-start | bytes 1572868 | tf_op jit(solution)/shard_map/while
  94.8 18.6 %copy-start.5 = (bf16[2,2048,64]{2,1,0:T(8,128)(2,1)}, bf16[2,2048,64]{2,1,0:T(8,128)(2,1)S(1)}, u32[]{:S(2)}) copy-start(bf16[2,2048,64]{2,1,0:T(8,128)(2,1)S(1)} %get-tuple-element.846) | copy-start | bytes 1572868
  94.8 7.7 copy-start.36
  99.0 12.8 %all-to-all-start.1 = ((bf16[4,2,32768]{2,1,0:T(2,128)(2,1)}), bf16[4,2,32768]{2,1,0:T(2,128)(2,1)S(1)}, u32[]{:S(2)}, u32[]{:S(2)}) async-start(bf16[4,2,32768]{2,1,0:T(2,128)(2,1)} %reshape.256), calls=%async_computation.1 | async-start | bytes 1048576 | tf_op jit(solution)/shard_map/all_to_all | solution.py:196
  102.5 101.8 %all-reduce.22.cloned.1.call-start = ((), (), s32[]{:S(2)}) async-start(), calls=%async_computation.8 | async-start | bytes 4194304 | tf_op jit(solution)/shard_map/psum | solution.py:77
  113.4 4.2 copy-start.56
  113.4 90.9 %copy-start.1 = (bf16[2,512,1024]{2,1,0:T(8,128)(2,1)S(1)}, bf16[2,512,1024]{2,1,0:T(8,128)(2,1)}, u32[]{:S(2)}) copy-start(bf16[2,512,1024]{2,1,0:T(8,128)(2,1)} %param.20) | copy-start | bytes 6291460
  116.4 93.5 %all-gather.4.cloned.1.call-start = ((), (), s32[]{:S(2)}) async-start(), calls=%async_computation.9 | async-start | bytes 3145728 | tf_op jit(solution)/shard_map/all_gather | solution.py:161
  117.0 100.3 %all-gather.6.cloned.1.call-start = ((), (), s32[]{:S(2)}) async-start(), calls=%async_computation.10 | async-start | bytes 3145728 | tf_op jit(solution)/shard_map/all_gather | solution.py:162
  117.5 206.5 %all-reduce.24.cloned.1.call-start = ((), (), s32[]{:S(2)}) async-start(), calls=%async_computation.11 | async-start | bytes 4194304 | tf_op jit(solution)/shard_map/psum | solution.py:77
  118.2 91.6 %copy-start.41 = (f32[1,1024]{1,0:T(1,128)}, f32[1,1024]{1,0:T(1,128)S(1)}, u32[]{:S(2)}) copy-start(f32[1,1024]{1,0:T(1,128)S(1)} %get-tuple-element.443) | copy-start | bytes 12292
  209.8 121.7 %copy-start.43 = (f32[1024]{0:T(1024)}, f32[1024]{0:T(1024)S(1)}, u32[]{:S(2)}) copy-start(f32[1024]{0:T(1024)S(1)} %fusion.66) | copy-start | bytes 12292
  209.9 7.4 copy-start.10
  209.9 7.4 copy-start.57
  217.3 17.7 %copy-start.63 = (bf16[1024,1024]{1,0:T(8,128)(2,1)S(1)}, bf16[1024,1024]{1,0:T(8,128)(2,1)}, u32[]{:S(2)}) copy-start(bf16[1024,1024]{1,0:T(8,128)(2,1)} %all-gather.4.cloned.1.call-done) | copy-start | bytes 6291460
  324.1 4.5 copy-start.4
  324.1 4.7 copy-start.7
  337.8 12.4 %all-to-all-start.2 = ((bf16[2,512,256]{1,0,2:T(2,128)(2,1)}), bf16[2,512,256]{1,0,2:T(2,128)(2,1)S(1)}, u32[]{:S(2)}, u32[]{:S(2)}) async-start(bf16[2,512,256]{1,0,2:T(2,128)(2,1)} %copy.79), calls=%async_computation.2 | async-start | bytes 1048576 | tf_op jit(solution)/shard_map/all_to_all | solution.py:233
  469.5 8.5 %copy-start.58 = (f32[1024]{0:T(1024)S(1)}, f32[1024]{0:T(1024)}, u32[]{:S(2)}) copy-start(f32[1024]{0:T(1024)} %param.26) | copy-start | bytes 12292
  472.8 24.5 %all-to-all-start.3 = ((bf16[4,2,98304]{2,1,0:T(2,128)(2,1)}), bf16[4,2,98304]{2,1,0:T(2,128)(2,1)}, u32[]{:S(2)}, u32[]{:S(2)}) async-start(bf16[4,2,98304]{2,1,0:T(2,128)(2,1)} %reshape.258), calls=%async_computation.3 | async-start | bytes 3145728 | tf_op jit(solution)/shard_map/all_to_all | solution.py:249
  477.2 38.7 %all-gather.8.cloned.1.call-start = ((), (), s32[]{:S(2)}) async-start(), calls=%async_computation.12 | async-start | bytes 2359296 | tf_op jit(solution)/shard_map/all_gather | solution.py:208
  477.7 196.1 %all-reduce.26.cloned.1.call-start = ((), (), s32[]{:S(2)}) async-start(), calls=%async_computation.17 | async-start | bytes 8388608 | tf_op jit(solution)/shard_map/psum | solution.py:77
  478.0 6.0 copy-start.62
  515.8 4.8 copy-start.19
  520.5 5.1 copy-start.11
  520.6 162.7 %reduce-scatter.7.cloned.1.call-start = ((), (), s32[]{:S(2)}) async-start(), calls=%async_computation.14 | async-start | bytes 786432 | tf_op jit(solution)/shard_map/reduce_scatter | solution.py:288
  525.3 5.9 copy-start.40
  525.3 5.9 copy-start.44
  525.3 5.9 copy-start.60
  525.3 157.9 %reduce-scatter.11.cloned.1.call-start = ((), (), s32[]{:S(2)}) async-start(), calls=%async_computation.16 | async-start | bytes 3145728 | tf_op jit(solution)/shard_map/reduce_scatter | solution.py:294
  531.1 7.1 copy-start.48
  531.1 7.1 copy-start.49
  531.1 142.8 %copy-start.2 = (bf16[2,512,1024]{2,1,0:T(8,128)(2,1)S(1)}, bf16[2,512,1024]{2,1,0:T(8,128)(2,1)}, u32[]{:S(2)}) copy-start(bf16[2,512,1024]{2,1,0:T(8,128)(2,1)} %param.20) | copy-start | bytes 6291460
  531.1 142.8 %copy-start.38 = (f32[1,1024]{1,0:T(1,128)S(1)}, f32[1,1024]{1,0:T(1,128)}, u32[]{:S(2)}) copy-start(f32[1,1024]{1,0:T(1,128)} %copy-done.37) | copy-start | bytes 12292
  531.1 152.2 %reduce-scatter.9.cloned.1.call-start = ((), (), s32[]{:S(2)}) async-start(), calls=%async_computation.15 | async-start | bytes 3145728 | tf_op jit(solution)/shard_map/reduce_scatter | solution.py:291
  538.1 138.9 %copy-start.46 = (f32[1,1024]{1,0:T(1,128)S(1)}, f32[1,1024]{1,0:T(1,128)}, u32[]{:S(2)}) copy-start(f32[1,1024]{1,0:T(1,128)} %copy-done.45) | copy-start | bytes 12292
  538.1 170.2 %reduce-scatter.5.cloned.1.call-start = ((), (), s32[]{:S(2)}) async-start(), calls=%async_computation.13 | async-start | bytes 2359296 | tf_op jit(solution)/shard_map/reduce_scatter | solution.py:285
  676.9 3.2 copy-start.18
  677.0 3.2 copy-start.20
  683.1 27.2 %copy-start.47 = (f32[1024]{0:T(1024)S(1)}, f32[1024]{0:T(1024)}, u32[]{:S(2)}) copy-start(f32[1024]{0:T(1024)} %get-tuple-element.369) | copy-start | bytes 12292
  683.1 28.5 %copy-start.50 = (f32[1024]{0:T(1024)S(1)}, f32[1024]{0:T(1024)}, u32[]{:S(2)}) copy-start(f32[1024]{0:T(1024)} %get-tuple-element.296) | copy-start | bytes 12292
  683.1 28.6 %copy-start.51 = (f32[1024]{0:T(1024)S(1)}, f32[1024]{0:T(1024)}, u32[]{:S(2)}) copy-start(f32[1024]{0:T(1024)} %get-tuple-element.290) | copy-start | bytes 12292
  683.1 28.6 %copy-start.61 = (f32[1024]{0:T(1024)S(1)}, f32[1024]{0:T(1024)}, u32[]{:S(2)}) copy-start(f32[1024]{0:T(1024)} %get-tuple-element.371) | copy-start | bytes 12292
  683.1 54.3 %copy-start.42 = (f32[1,1024]{1,0:T(1,128)S(1)}, f32[1,1024]{1,0:T(1,128)}, u32[]{:S(2)}) copy-start(f32[1,1024]{1,0:T(1,128)} %copy-done.41) | copy-start | bytes 12292
  683.1 54.3 %copy-start.52 = (f32[1,1024]{1,0:T(1,128)S(1)}, f32[1,1024]{1,0:T(1,128)}, u32[]{:S(2)}) copy-start(f32[1,1024]{1,0:T(1,128)} %get-tuple-element.442) | copy-start | bytes 12292
  683.2 94.4 %all-reduce.28.cloned.1.call-start = ((), (), s32[]{:S(2)}) async-start(), calls=%async_computation.18 | async-start | bytes 6291456 | tf_op jit(solution)/shard_map/psum | solution.py:299
  777.6 7.2 copy-start.33
  (20 other events, 36.5 us)
Sparse Core Ops, SparseCore 0:
  116.5 87.7 all-reduce.21
  238.9 85.1 all-reduce.23
  520.7 153.1 all-reduce.25
  708.5 69.0 all-reduce.27
Sparse Core Ops, SparseCore 1:
  118.4 34.5 all-gather.3
  154.4 32.9 all-gather.5
  479.2 26.5 all-gather.7
  525.4 12.7 reduce-scatter.6
  540.4 31.8 reduce-scatter.10
  574.5 31.8 reduce-scatter.8
  683.3 25.0 reduce-scatter.4
